TPU v7x, 128 devices: a whole 4x4x4 slice. The times are simulated.
128 devices in a mesh: blk: 32 (over y, z, x_hi), tab: 4 (over x_lo, core).
Axes of the slice: x: 4 (x_hi: 2, x_lo: 2; x = x_hi * 2 + x_lo), y: 4, z: 4, core: 2. Of those that a mesh axis runs over, the one named last changes fastest.
Arguments:
- accounts: bfloat16 [262144, 128], P(('blk', 'tab')), may hold values from -0.5 to 0.5
- merchants: bfloat16 [262144, 128], P(('blk', 'tab')), may hold values from -6 to 6
- logit_scale: float32 [1], replicated, may hold values from 1 to 4
- logit_bias: float32 [1], replicated, may hold values from -3 to -1
- positive: int32 [262144], P(('blk', 'tab')), may hold values from 0 to 8191
- account_ids: int32 [262144], P(('blk', 'tab')), may hold values from 0 to 1023
- merchant_ids: int32 [262144], P(('blk', 'tab')), may hold values from 0 to 1023
- account_owner: int32 [2048, 1], P(('blk', 'tab')), may hold values from 0 to 3; in each aligned block of 16 rows (0 to 15, 16 to 31, ...) at most 8 rows name the same one
- merchant_owner: int32 [2048, 1], P(('blk', 'tab')), may hold values from 0 to 3; in each aligned block of 16 rows (0 to 15, 16 to 31, ...) at most 8 rows name the same one
Outputs:
- account_grad: float32 [131072, 128], P(('blk', 'tab'))
- merchant_grad: float32 [131072, 128], P(('blk', 'tab'))
Inputs may be any that keep to these rules, and one draw needn't show every extreme that they name: `account_owner`: among the 16 row blocks of one batch block at most 8 have the same owner, and some batch block gives exactly 8 to one owner. `merchant_owner`: among the 16 row blocks of one batch block at most 8 have the same owner, and some batch block gives exactly 8 to one owner.
All inputs are finite; a program needn't handle non-finite values.
Results may differ from a plain program's by a relative error of at most 0.00048.
Values may be sent and summed in bfloat16 or wider, within the bound.
No kernel may reach another device: no remote copies, remote signals or barrier semaphores. Data moves between devices by JAX's collectives and lax.ppermute only.
A program may use at most 64 MiB of HBM per device.

v0:
```python
import jax
import jax.numpy as jnp
from jax import lax
from jax.sharding import PartitionSpec as P

D = 128
STEPS = 4
BLOCK_ROWS = 128
TROWS = 1024


def shifted(block, axis, distance):
    devices = range(lax.axis_size(axis))
    route = [((i - distance) % len(devices), i) for i in devices]
    return lax.ppermute(block, axis, route)


def score_delta(piece, label, merch_block, columns, scale, bias):
    logits = (
        scale
        * lax.dot_general(
            piece, merch_block, (((1,), (1,)), ((), ())), preferred_element_type=jnp.float32
        )
        + bias
    )
    signs = jnp.where(label[:, None] == columns[None, :], jnp.float32(1.0), jnp.float32(-1.0))
    return (-signs * jax.nn.sigmoid(-signs * logits)).astype(jnp.bfloat16)


def tile_grads(acc_block, merch_block, relative, scale, bias):
    row_count = acc_block.shape[0]
    row_step = min(512, row_count)
    count = row_count // row_step
    pieces = acc_block.reshape(count, row_step, D)
    labels = relative.reshape(count, row_step)
    columns = jnp.arange(merch_block.shape[0], dtype=jnp.int32)

    def tile_one_block(carry, item):
        piece, label = item
        delta = score_delta(piece, label, merch_block, columns, scale, bias)
        grad_rows = scale * jnp.dot(delta, merch_block, preferred_element_type=jnp.float32)
        merch_part = carry + scale * lax.dot_general(
            delta, piece, (((0,), (0,)), ((), ())), preferred_element_type=jnp.float32
        )
        return (merch_part, grad_rows)

    start = jnp.zeros((merch_block.shape[0], D), jnp.float32)
    merch_grad, acc_grad = lax.scan(tile_one_block, start, (pieces, labels))
    return (acc_grad.reshape(-1, D), merch_grad)


def account_only(acc_block, merch_block, relative, offset, scale, bias):
    row_count = acc_block.shape[0]
    row_step = min(512, row_count)
    count = row_count // row_step
    pieces = acc_block.reshape(count, row_step, D)
    labels = relative.reshape(count, row_step)
    columns = offset + jnp.arange(merch_block.shape[0], dtype=jnp.int32)

    def account_one_block(item):
        piece, label = item
        delta = score_delta(piece, label, merch_block, columns, scale, bias)
        return scale * jnp.dot(delta, merch_block, preferred_element_type=jnp.float32)

    return lax.map(account_one_block, (pieces, labels)).reshape(-1, D)


def merchant_only(acc_block, merch_block, relative, offset, scale, bias):
    row_count = acc_block.shape[0]
    row_step = min(512, row_count)
    count = row_count // row_step
    pieces = acc_block.reshape(count, row_step, D)
    labels = relative.reshape(count, row_step)
    columns = offset + jnp.arange(merch_block.shape[0], dtype=jnp.int32)

    def merchant_one_block(carry, item):
        piece, label = item
        delta = score_delta(piece, label, merch_block, columns, scale, bias)
        return (
            carry
            + scale
            * lax.dot_general(
                delta, piece, (((0,), (0,)), ((), ())), preferred_element_type=jnp.float32
            ),
            None,
        )

    start = jnp.zeros((merch_block.shape[0], D), jnp.float32)
    merch_grad, unused = lax.scan(merchant_one_block, start, (pieces, labels))
    return merch_grad


def pack_blocks(grads, ids, owner, owners_count):
    owner_list = owner[:, 0]
    block_count = owner_list.shape[0]
    capacity = block_count // 2
    lanes = jnp.arange(owners_count, dtype=jnp.int32)
    hitting = (owner_list[:, None] == lanes[None, :]).astype(jnp.int32)
    earlier = jnp.cumsum(hitting, axis=0) - hitting
    ranking = jnp.sum(earlier * hitting, axis=1)
    placing = owner_list * capacity + ranking
    slots = jnp.arange(owners_count * capacity, dtype=jnp.int32)
    matching = placing[None, :] == slots[:, None]
    filled = jnp.any(matching, axis=1)
    source = jnp.argmax(matching, axis=1)
    payload = jnp.take(grads.reshape(block_count, BLOCK_ROWS, D), source, axis=0)
    payload = jnp.where(filled[:, None, None], payload, jnp.float32(0.0))
    row_keys = jnp.take(ids.reshape(block_count, BLOCK_ROWS), source, axis=0)
    row_keys = jnp.where(filled[:, None], row_keys, 0)
    return (
        payload.reshape(owners_count, capacity, BLOCK_ROWS, D),
        row_keys.reshape(owners_count, capacity, BLOCK_ROWS),
    )


def per_device(
    accounts,
    merchants,
    logit_scale,
    logit_bias,
    positive,
    account_ids,
    merchant_ids,
    account_owner,
    merchant_owner,
):
    scale = logit_scale[0]
    bias = logit_bias[0]
    row_count = accounts.shape[0]
    acc_grad, merch_grad = tile_grads(accounts, merchants, positive, scale, bias)
    visiting = merchants
    guest_rows = accounts
    guest_labels = positive
    for cycle_step in range(1, STEPS):
        visiting = shifted(visiting, "blk", 1)
        guest_rows, guest_labels = shifted((guest_rows, guest_labels), "blk", -1)
        acc_grad = acc_grad + account_only(
            accounts, visiting, positive, cycle_step * row_count, scale, bias
        )
        merch_grad = merch_grad + merchant_only(
            guest_rows, merchants, guest_labels, cycle_step * row_count, scale, bias
        )
    owners_count = lax.axis_size("tab")
    acc_payload, acc_keys = pack_blocks(acc_grad, account_ids, account_owner, owners_count)
    merch_payload, merch_keys = pack_blocks(merch_grad, merchant_ids, merchant_owner, owners_count)
    acc_payload, acc_keys, merch_payload, merch_keys = (
        lax.all_to_all(acc_payload, "tab", split_axis=0, concat_axis=0, tiled=True),
        lax.all_to_all(acc_keys, "tab", split_axis=0, concat_axis=0, tiled=True),
        lax.all_to_all(merch_payload, "tab", split_axis=0, concat_axis=0, tiled=True),
        lax.all_to_all(merch_keys, "tab", split_axis=0, concat_axis=0, tiled=True),
    )
    account_grad = jax.ops.segment_sum(
        acc_payload.reshape(-1, D), acc_keys.reshape(-1), num_segments=TROWS
    )
    merchant_grad = jax.ops.segment_sum(
        merch_payload.reshape(-1, D), merch_keys.reshape(-1), num_segments=TROWS
    )
    return (account_grad, merchant_grad)


def solution(mesh):
    return jax.shard_map(
        per_device,
        mesh=mesh,
        in_specs=(
            P(("blk", "tab"), None),
            P(("blk", "tab"), None),
            P(),
            P(),
            P(("blk", "tab")),
            P(("blk", "tab")),
            P(("blk", "tab")),
            P(("blk", "tab"), None),
            P(("blk", "tab"), None),
        ),
        out_specs=(P(("blk", "tab"), None), P(("blk", "tab"), None)),
        check_vma=False,
    )
```

profile of v0, /device:TPU:3, one launch (start us, length us, event | category | flops | bytes accessed | tf_op | source)
XLA Modules:
  0.0 298.5 jit_solution(7579728464102849319)
XLA Ops:
  6.8 5.8 %all-to-all-start = ((s32[4,8,128]{2,1,0:T(8,128)}), s32[4,8,128]{2,1,0:T(8,128)}, u32[]{:S(2)}, u32[]{:S(2)}) async-start(s32[4,8,128]{2,1,0:T(8,128)} %fusion.91), calls=%async_computation | async-start | bytes 32768 | tf_op jit(solution)/shard_map/all_to_all | solution.py:148
  12.6 5.1 %collective-permute-start.4 = (bf16[2048,128]{1,0:T(8,128)(2,1)}, bf16[2048,128]{1,0:T(8,128)(2,1)}, u32[]{:S(2)}, u32[]{:S(2)}) collective-permute-start(bf16[2048,128]{1,0:T(8,128)(2,1)} %param.27), channel_id=1, source_target_pairs={{4,0},{8,4},{12,8},{16,12},{20,16},{24,20},{28,24},{32,28},{36,32}... | collective-permute-start | bytes 1572872 | tf_op jit(solution)/shard_map/ppermute | solution.py:15
  17.7 3.8 %collective-permute-start.3 = (s32[2048]{0:T(1024)}, s32[2048]{0:T(1024)S(1)}, u32[]{:S(2)}, u32[]{:S(2)}) collective-permute-start(s32[2048]{0:T(1024)} %param.31), channel_id=1, source_target_pairs={{4,0},{8,4},{12,8},{16,12},{20,16},{24,20},{28,24},{32,28},{36,32}... | collective-permute-start | bytes 24584 | tf_op jit(solution)/shard_map/ppermute | solution.py:15
  23.3 37.1 %while.82 = (s32[]{:T(128)}, f32[2048,128]{1,0:T(8,128)S(1)}, f32[4,512,128]{2,1,0:T(8,128)}, f32[]{:T(128)}, s32[4,512]{1,0:T(4,128)S(1)}, /*index=5*/bf16[4,51...) while((s32[]{:T(128)}, f32[2048,128]{1,0:T(8,128)S(1)}, ...), condition=%wide.region_5.7_spmd.clone, body=%wide.region_4.6_spmd.clone.sunk | while | flops 817692672 | bytes 12068495 | solution.py:48
  23.4 4.4 %multiply_convert_fusion.8 = bf16[512,2048]{1,0:T(8,128)(2,1)S(1)} fusion(bf16[2048,128]{1,0:T(8,128)(2,1)} %get-tuple-element.952, f32[]{:T(128)} %get-tuple-element.953, f32[]{:T(128)} %get-tuple-element.949, s32[512]{0:T(512)S(1)} %bitcast.171, bf16[4,512,128]{2,1,0:T(8,128)(2,1)} %get-tuple-element.951, s32[]{:T(128)} %get-tuple-element.936), kind=kOutput, calls=%fused_computation.50.clone.1 | convolution fusion | flops 279969792 | bytes 2756096 | tf_op jit(solution)/shard_map/while/body/eval_jaxpr/dot_general | solution.py:21
  32.7 4.4 %multiply_convert_fusion.8 = bf16[512,2048]{1,0:T(8,128)(2,1)S(1)} fusion(bf16[2048,128]{1,0:T(8,128)(2,1)} %get-tuple-element.952, f32[]{:T(128)} %get-tuple-element.953, f32[]{:T(128)} %get-tuple-element.949, s32[512]{0:T(512)S(1)} %bitcast.171, bf16[4,512,128]{2,1,0:T(8,128)(2,1)} %get-tuple-element.951, s32[]{:T(128)} %get-tuple-element.936), kind=kOutput, calls=%fused_computation.50.clone.1 | convolution fusion | flops 279969792 | bytes 2756096 | tf_op jit(solution)/shard_map/while/body/eval_jaxpr/dot_general | solution.py:21
  41.9 4.4 %multiply_convert_fusion.8 = bf16[512,2048]{1,0:T(8,128)(2,1)S(1)} fusion(bf16[2048,128]{1,0:T(8,128)(2,1)} %get-tuple-element.952, f32[]{:T(128)} %get-tuple-element.953, f32[]{:T(128)} %get-tuple-element.949, s32[512]{0:T(512)S(1)} %bitcast.171, bf16[4,512,128]{2,1,0:T(8,128)(2,1)} %get-tuple-element.951, s32[]{:T(128)} %get-tuple-element.936), kind=kOutput, calls=%fused_computation.50.clone.1 | convolution fusion | flops 279969792 | bytes 2756096 | tf_op jit(solution)/shard_map/while/body/eval_jaxpr/dot_general | solution.py:21
  51.2 4.4 %multiply_convert_fusion.8 = bf16[512,2048]{1,0:T(8,128)(2,1)S(1)} fusion(bf16[2048,128]{1,0:T(8,128)(2,1)} %get-tuple-element.952, f32[]{:T(128)} %get-tuple-element.953, f32[]{:T(128)} %get-tuple-element.949, s32[512]{0:T(512)S(1)} %bitcast.171, bf16[4,512,128]{2,1,0:T(8,128)(2,1)} %get-tuple-element.951, s32[]{:T(128)} %get-tuple-element.936), kind=kOutput, calls=%fused_computation.50.clone.1 | convolution fusion | flops 279969792 | bytes 2756096 | tf_op jit(solution)/shard_map/while/body/eval_jaxpr/dot_general | solution.py:21
  65.6 4.7 %collective-permute-start.7 = (s32[2048]{0:T(1024)S(1)}, s32[2048]{0:T(1024)S(1)}, u32[]{:S(2)}, u32[]{:S(2)}) collective-permute-start(s32[2048]{0:T(1024)S(1)} %collective-permute-done.5), channel_id=1, source_target_pairs={{4,0},{8,4},{12,8},{16,12},{20,16},{24,20},{28,24},{32,28},{36,32}... | collective-permute-start | bytes 24584 | tf_op jit(solution)/shard_map/ppermute | solution.py:15
  71.8 20.7 %while.83 = (s32[]{:T(128)}, f32[2048,128]{1,0:T(8,128)S(1)}, f32[]{:T(128)}, s32[4,512]{1,0:T(4,128)S(1)}, bf16[4,512,128]{2,1,0:T(8,128)(2,1)}, /*index=5*/bf1...) while((s32[]{:T(128)}, f32[2048,128]{1,0:T(8,128)S(1)}, f32[]{:T(128)}, ...), condition=%wide.region_18.21_spmd.clone, body=%wide.region_17.20_spmd.clone.sunk | while | flops 549193728 | bytes 2908779 | solution.py:89
  71.8 5.2 %fusion.164 = f32[2048,128]{1,0:T(8,128)S(1)} fusion(bf16[2048,128]{1,0:T(8,128)(2,1)} %get-tuple-element.1057, f32[]{:T(128)} %get-tuple-element.1058, f32[]{:T(128)} %get-tuple-element.1054, s32[2048]{0:T(1024)S(1)} %iota_add_fusion.15, s32[512]{0:T(512)S(1)} %bitcast.165, f32[2048,128]{1,0:T(8,128)S(1)} %get-tuple-element.1044, ...), kind=kOutput, calls=%fused_computation.65.clone.1 | convolution fusion | flops 549191680 | bytes 2896385 | tf_op jit(solution)/shard_map/while/body/eval_jaxpr/dot_general | solution.py:82
  77.0 5.1 %fusion.164 = f32[2048,128]{1,0:T(8,128)S(1)} fusion(bf16[2048,128]{1,0:T(8,128)(2,1)} %get-tuple-element.1057, f32[]{:T(128)} %get-tuple-element.1058, f32[]{:T(128)} %get-tuple-element.1054, s32[2048]{0:T(1024)S(1)} %iota_add_fusion.15, s32[512]{0:T(512)S(1)} %bitcast.165, f32[2048,128]{1,0:T(8,128)S(1)} %get-tuple-element.1044, ...), kind=kOutput, calls=%fused_computation.65.clone.1 | convolution fusion | flops 549191680 | bytes 2896385 | tf_op jit(solution)/shard_map/while/body/eval_jaxpr/dot_general | solution.py:82
  82.2 5.1 %fusion.164 = f32[2048,128]{1,0:T(8,128)S(1)} fusion(bf16[2048,128]{1,0:T(8,128)(2,1)} %get-tuple-element.1057, f32[]{:T(128)} %get-tuple-element.1058, f32[]{:T(128)} %get-tuple-element.1054, s32[2048]{0:T(1024)S(1)} %iota_add_fusion.15, s32[512]{0:T(512)S(1)} %bitcast.165, f32[2048,128]{1,0:T(8,128)S(1)} %get-tuple-element.1044, ...), kind=kOutput, calls=%fused_computation.65.clone.1 | convolution fusion | flops 549191680 | bytes 2896385 | tf_op jit(solution)/shard_map/while/body/eval_jaxpr/dot_general | solution.py:82
  87.3 5.1 %fusion.164 = f32[2048,128]{1,0:T(8,128)S(1)} fusion(bf16[2048,128]{1,0:T(8,128)(2,1)} %get-tuple-element.1057, f32[]{:T(128)} %get-tuple-element.1058, f32[]{:T(128)} %get-tuple-element.1054, s32[2048]{0:T(1024)S(1)} %iota_add_fusion.15, s32[512]{0:T(512)S(1)} %bitcast.165, f32[2048,128]{1,0:T(8,128)S(1)} %get-tuple-element.1044, ...), kind=kOutput, calls=%fused_computation.65.clone.1 | convolution fusion | flops 549191680 | bytes 2896385 | tf_op jit(solution)/shard_map/while/body/eval_jaxpr/dot_general | solution.py:82
  92.5 7.5 %collective-permute-start.6 = (bf16[2048,128]{1,0:T(8,128)(2,1)}, bf16[2048,128]{1,0:T(8,128)(2,1)}, u32[]{:S(2)}, u32[]{:S(2)}) collective-permute-start(bf16[2048,128]{1,0:T(8,128)(2,1)} %collective-permute-done.4), channel_id=1, source_target_pairs={{4,0},{8,4},{12,8},{16,12},{20,16},{24,20},{28,24},{32,28},{36,32}... | collective-permute-start | bytes 1572872 | tf_op jit(solution)/shard_map/ppermute | solution.py:15
  100.1 18.2 %while.79 = (s32[]{:T(128)}, f32[4,512,128]{2,1,0:T(8,128)S(1)}, f32[]{:T(128)}, s32[4,512]{1,0:T(4,128)S(1)}, bf16[4,512,128]{2,1,0:T(8,128)(2,1)S(1)}, /*index=5*/bf16[2048,128]{1,0:T(8,128)(2,1)}, f32[]{:T(128)}, s32[]{:T(128)}) while((s32[]{:T(128)}, f32[4,512,128]{2,1,0:T(8,128)S(1)}, f32[]{:T(128)}, s32[4,512]{1,0:T(4,128)S(1)}, ...), condition=%wide.region_7.9_spmd.clone, body=%wide.region_6.8_spmd.clone.sunk | while | flops 548472832 | bytes 1466969 | solution.py:65
  100.1 4.6 %fusion.144 = f32[4,512,128]{2,1,0:T(8,128)S(1)} fusion(f32[4,512,128]{2,1,0:T(8,128)S(1)} %get-tuple-element.965, s32[]{:T(128)} %get-tuple-element.964, bf16[2048,128]{1,0:T(8,128)(2,1)} %get-tuple-element.977, f32[]{:T(128)} %get-tuple-element.978, f32[]{:T(128)} %get-tuple-element.974, s32[2048]{0:T(1024)S(1)} %iota_add_fusion.12, ...), kind=kOutput, calls=%fused_computation.17.clone.1 | convolution fusion | flops 548470784 | bytes 1454592 | tf_op jit(solution)/shard_map/while/body/eval_jaxpr/dot_general | solution.py:63
  104.8 4.5 %fusion.144 = f32[4,512,128]{2,1,0:T(8,128)S(1)} fusion(f32[4,512,128]{2,1,0:T(8,128)S(1)} %get-tuple-element.965, s32[]{:T(128)} %get-tuple-element.964, bf16[2048,128]{1,0:T(8,128)(2,1)} %get-tuple-element.977, f32[]{:T(128)} %get-tuple-element.978, f32[]{:T(128)} %get-tuple-element.974, s32[2048]{0:T(1024)S(1)} %iota_add_fusion.12, ...), kind=kOutput, calls=%fused_computation.17.clone.1 | convolution fusion | flops 548470784 | bytes 1454592 | tf_op jit(solution)/shard_map/while/body/eval_jaxpr/dot_general | solution.py:63
  109.3 4.5 %fusion.144 = f32[4,512,128]{2,1,0:T(8,128)S(1)} fusion(f32[4,512,128]{2,1,0:T(8,128)S(1)} %get-tuple-element.965, s32[]{:T(128)} %get-tuple-element.964, bf16[2048,128]{1,0:T(8,128)(2,1)} %get-tuple-element.977, f32[]{:T(128)} %get-tuple-element.978, f32[]{:T(128)} %get-tuple-element.974, s32[2048]{0:T(1024)S(1)} %iota_add_fusion.12, ...), kind=kOutput, calls=%fused_computation.17.clone.1 | convolution fusion | flops 548470784 | bytes 1454592 | tf_op jit(solution)/shard_map/while/body/eval_jaxpr/dot_general | solution.py:63
  113.8 4.5 %fusion.144 = f32[4,512,128]{2,1,0:T(8,128)S(1)} fusion(f32[4,512,128]{2,1,0:T(8,128)S(1)} %get-tuple-element.965, s32[]{:T(128)} %get-tuple-element.964, bf16[2048,128]{1,0:T(8,128)(2,1)} %get-tuple-element.977, f32[]{:T(128)} %get-tuple-element.978, f32[]{:T(128)} %get-tuple-element.974, s32[2048]{0:T(1024)S(1)} %iota_add_fusion.12, ...), kind=kOutput, calls=%fused_computation.17.clone.1 | convolution fusion | flops 548470784 | bytes 1454592 | tf_op jit(solution)/shard_map/while/body/eval_jaxpr/dot_general | solution.py:63
  118.6 20.1 %while.84 = (s32[]{:T(128)}, f32[2048,128]{1,0:T(8,128)S(1)}, f32[]{:T(128)}, s32[4,512]{1,0:T(4,128)S(1)}, bf16[4,512,128]{2,1,0:T(8,128)(2,1)}, /*index=5*/bf1...) while((s32[]{:T(128)}, f32[2048,128]{1,0:T(8,128)S(1)}, f32[]{:T(128)}, ...), condition=%wide.region_20.23_spmd.clone, body=%wide.region_19.22_spmd.clone.sunk | while | flops 549193728 | bytes 2908779 | solution.py:89
  118.7 5.0 %fusion.168 = f32[2048,128]{1,0:T(8,128)S(1)} fusion(bf16[2048,128]{1,0:T(8,128)(2,1)S(1)} %get-tuple-element.1030, f32[]{:T(128)} %get-tuple-element.1031, f32[]{:T(128)} %get-tuple-element.1027, s32[2048]{0:T(1024)S(1)} %iota_add_fusion.16, s32[512]{0:T(512)S(1)} %bitcast.166, f32[2048,128]{1,0:T(8,128)S(1)} %get-tuple-element.1017, ...), kind=kOutput, calls=%fused_computation.75.clone.1 | convolution fusion | flops 549191680 | bytes 2896385 | tf_op jit(solution)/shard_map/while/body/eval_jaxpr/dot_general | solution.py:82
  123.7 5.0 %fusion.168 = f32[2048,128]{1,0:T(8,128)S(1)} fusion(bf16[2048,128]{1,0:T(8,128)(2,1)S(1)} %get-tuple-element.1030, f32[]{:T(128)} %get-tuple-element.1031, f32[]{:T(128)} %get-tuple-element.1027, s32[2048]{0:T(1024)S(1)} %iota_add_fusion.16, s32[512]{0:T(512)S(1)} %bitcast.166, f32[2048,128]{1,0:T(8,128)S(1)} %get-tuple-element.1017, ...), kind=kOutput, calls=%fused_computation.75.clone.1 | convolution fusion | flops 549191680 | bytes 2896385 | tf_op jit(solution)/shard_map/while/body/eval_jaxpr/dot_general | solution.py:82
  128.7 5.0 %fusion.168 = f32[2048,128]{1,0:T(8,128)S(1)} fusion(bf16[2048,128]{1,0:T(8,128)(2,1)S(1)} %get-tuple-element.1030, f32[]{:T(128)} %get-tuple-element.1031, f32[]{:T(128)} %get-tuple-element.1027, s32[2048]{0:T(1024)S(1)} %iota_add_fusion.16, s32[512]{0:T(512)S(1)} %bitcast.166, f32[2048,128]{1,0:T(8,128)S(1)} %get-tuple-element.1017, ...), kind=kOutput, calls=%fused_computation.75.clone.1 | convolution fusion | flops 549191680 | bytes 2896385 | tf_op jit(solution)/shard_map/while/body/eval_jaxpr/dot_general | solution.py:82
  133.8 5.0 %fusion.168 = f32[2048,128]{1,0:T(8,128)S(1)} fusion(bf16[2048,128]{1,0:T(8,128)(2,1)S(1)} %get-tuple-element.1030, f32[]{:T(128)} %get-tuple-element.1031, f32[]{:T(128)} %get-tuple-element.1027, s32[2048]{0:T(1024)S(1)} %iota_add_fusion.16, s32[512]{0:T(512)S(1)} %bitcast.166, f32[2048,128]{1,0:T(8,128)S(1)} %get-tuple-element.1017, ...), kind=kOutput, calls=%fused_computation.75.clone.1 | convolution fusion | flops 549191680 | bytes 2896385 | tf_op jit(solution)/shard_map/while/body/eval_jaxpr/dot_general | solution.py:82
  139.8 18.1 %while.80 = (s32[]{:T(128)}, f32[4,512,128]{2,1,0:T(8,128)S(1)}, f32[]{:T(128)}, s32[4,512]{1,0:T(4,128)S(1)}, bf16[4,512,128]{2,1,0:T(8,128)(2,1)S(1)}, /*index=5*/bf16[2048,128]{1,0:T(8,128)(2,1)}, f32[]{:T(128)}, s32[]{:T(128)}) while((s32[]{:T(128)}, f32[4,512,128]{2,1,0:T(8,128)S(1)}, f32[]{:T(128)}, ...), condition=%wide.region_9.11_spmd.clone, body=%wide.region_8.10_spmd.clone.sunk | while | flops 548472832 | bytes 1466969 | solution.py:65
  139.9 4.5 %fusion.148 = f32[4,512,128]{2,1,0:T(8,128)S(1)} fusion(f32[4,512,128]{2,1,0:T(8,128)S(1)} %get-tuple-element.911, s32[]{:T(128)} %get-tuple-element.910, bf16[2048,128]{1,0:T(8,128)(2,1)} %get-tuple-element.923, f32[]{:T(128)} %get-tuple-element.924, f32[]{:T(128)} %get-tuple-element.920, s32[2048]{0:T(1024)S(1)} %iota_add_fusion.13, ...), kind=kOutput, calls=%fused_computation.29.clone.1 | convolution fusion | flops 548470784 | bytes 1454592 | tf_op jit(solution)/shard_map/while/body/eval_jaxpr/dot_general | solution.py:63
  144.4 4.5 %fusion.148 = f32[4,512,128]{2,1,0:T(8,128)S(1)} fusion(f32[4,512,128]{2,1,0:T(8,128)S(1)} %get-tuple-element.911, s32[]{:T(128)} %get-tuple-element.910, bf16[2048,128]{1,0:T(8,128)(2,1)} %get-tuple-element.923, f32[]{:T(128)} %get-tuple-element.924, f32[]{:T(128)} %get-tuple-element.920, s32[2048]{0:T(1024)S(1)} %iota_add_fusion.13, ...), kind=kOutput, calls=%fused_computation.29.clone.1 | convolution fusion | flops 548470784 | bytes 1454592 | tf_op jit(solution)/shard_map/while/body/eval_jaxpr/dot_general | solution.py:63
  148.9 4.5 %fusion.148 = f32[4,512,128]{2,1,0:T(8,128)S(1)} fusion(f32[4,512,128]{2,1,0:T(8,128)S(1)} %get-tuple-element.911, s32[]{:T(128)} %get-tuple-element.910, bf16[2048,128]{1,0:T(8,128)(2,1)} %get-tuple-element.923, f32[]{:T(128)} %get-tuple-element.924, f32[]{:T(128)} %get-tuple-element.920, s32[2048]{0:T(1024)S(1)} %iota_add_fusion.13, ...), kind=kOutput, calls=%fused_computation.29.clone.1 | convolution fusion | flops 548470784 | bytes 1454592 | tf_op jit(solution)/shard_map/while/body/eval_jaxpr/dot_general | solution.py:63
  153.5 4.5 %fusion.148 = f32[4,512,128]{2,1,0:T(8,128)S(1)} fusion(f32[4,512,128]{2,1,0:T(8,128)S(1)} %get-tuple-element.911, s32[]{:T(128)} %get-tuple-element.910, bf16[2048,128]{1,0:T(8,128)(2,1)} %get-tuple-element.923, f32[]{:T(128)} %get-tuple-element.924, f32[]{:T(128)} %get-tuple-element.920, s32[2048]{0:T(1024)S(1)} %iota_add_fusion.13, ...), kind=kOutput, calls=%fused_computation.29.clone.1 | convolution fusion | flops 548470784 | bytes 1454592 | tf_op jit(solution)/shard_map/while/body/eval_jaxpr/dot_general | solution.py:63
  158.0 7.3 %collective-permute-start.8 = (bf16[2048,128]{1,0:T(8,128)(2,1)}, bf16[2048,128]{1,0:T(8,128)(2,1)}, u32[]{:S(2)}, u32[]{:S(2)}) collective-permute-start(bf16[2048,128]{1,0:T(8,128)(2,1)} %collective-permute-done.6), channel_id=1, source_target_pairs={{4,0},{8,4},{12,8},{16,12},{20,16},{24,20},{28,24},{32,28},{36,32}... | collective-permute-start | bytes 1572872 | tf_op jit(solution)/shard_map/ppermute | solution.py:15
  166.3 20.8 %while.81 = (s32[]{:T(128)}, f32[4,512,128]{2,1,0:T(8,128)}, f32[]{:T(128)}, s32[4,512]{1,0:T(4,128)S(1)}, bf16[4,512,128]{2,1,0:T(8,128)(2,1)S(1)}, /*index=5*/bf16[2048,128]{1,0:T(8,128)(2,1)}, f32[]{:T(128)}, s32[]{:T(128)}) while((s32[]{:T(128)}, f32[4,512,128]{2,1,0:T(8,128)}, f32[]{:T(128)}, s32[4,512]{1,0:T(4,128)S(1)}, ...), condition=%wide.region_11.13_spmd.clone, body=%wide.region_10.12_spmd.clone.sunk | while | flops 548472832 | bytes 1466969 | solution.py:65
  166.4 5.2 %fusion.152 = f32[4,512,128]{2,1,0:T(8,128)} fusion(f32[4,512,128]{2,1,0:T(8,128)} %get-tuple-element.887, s32[]{:T(128)} %get-tuple-element.886, bf16[2048,128]{1,0:T(8,128)(2,1)} %get-tuple-element.899, f32[]{:T(128)} %get-tuple-element.900, f32[]{:T(128)} %get-tuple-element.896, s32[2048]{0:T(1024)S(1)} %iota_add_fusion.14, ...), kind=kOutput, calls=%fused_computation.41.clone.1 | convolution fusion | flops 548470784 | bytes 1454592 | tf_op jit(solution)/shard_map/while/body/eval_jaxpr/dot_general | solution.py:63
  171.6 5.2 %fusion.152 = f32[4,512,128]{2,1,0:T(8,128)} fusion(f32[4,512,128]{2,1,0:T(8,128)} %get-tuple-element.887, s32[]{:T(128)} %get-tuple-element.886, bf16[2048,128]{1,0:T(8,128)(2,1)} %get-tuple-element.899, f32[]{:T(128)} %get-tuple-element.900, f32[]{:T(128)} %get-tuple-element.896, s32[2048]{0:T(1024)S(1)} %iota_add_fusion.14, ...), kind=kOutput, calls=%fused_computation.41.clone.1 | convolution fusion | flops 548470784 | bytes 1454592 | tf_op jit(solution)/shard_map/while/body/eval_jaxpr/dot_general | solution.py:63
  176.8 5.2 %fusion.152 = f32[4,512,128]{2,1,0:T(8,128)} fusion(f32[4,512,128]{2,1,0:T(8,128)} %get-tuple-element.887, s32[]{:T(128)} %get-tuple-element.886, bf16[2048,128]{1,0:T(8,128)(2,1)} %get-tuple-element.899, f32[]{:T(128)} %get-tuple-element.900, f32[]{:T(128)} %get-tuple-element.896, s32[2048]{0:T(1024)S(1)} %iota_add_fusion.14, ...), kind=kOutput, calls=%fused_computation.41.clone.1 | convolution fusion | flops 548470784 | bytes 1454592 | tf_op jit(solution)/shard_map/while/body/eval_jaxpr/dot_general | solution.py:63
  182.0 5.2 %fusion.152 = f32[4,512,128]{2,1,0:T(8,128)} fusion(f32[4,512,128]{2,1,0:T(8,128)} %get-tuple-element.887, s32[]{:T(128)} %get-tuple-element.886, bf16[2048,128]{1,0:T(8,128)(2,1)} %get-tuple-element.899, f32[]{:T(128)} %get-tuple-element.900, f32[]{:T(128)} %get-tuple-element.896, s32[2048]{0:T(1024)S(1)} %iota_add_fusion.14, ...), kind=kOutput, calls=%fused_computation.41.clone.1 | convolution fusion | flops 548470784 | bytes 1454592 | tf_op jit(solution)/shard_map/while/body/eval_jaxpr/dot_general | solution.py:63
  191.5 7.6 %all-to-all-start.2 = ((s32[4,8,128]{2,1,0:T(8,128)}), s32[4,8,128]{2,1,0:T(8,128)S(1)}, u32[]{:S(2)}, u32[]{:S(2)}) async-start(s32[4,8,128]{2,1,0:T(8,128)} %fusion.90), calls=%async_computation.2 | async-start | bytes 32768 | tf_op jit(solution)/shard_map/all_to_all | solution.py:150
  199.1 3.2 %select_select_fusion.1 = f32[32,128,128]{2,1,0:T(8,128)} fusion(f32[32,128,128]{2,1,0:T(8,128)} %gather_fusion.1, pred[32]{0:T(512)(128)(4,1)S(1)} %copy-done.16, pred[32]{0:T(512)(128)(4,1)S(1)} %copy-done.18), kind=kLoop, calls=%fused_computation.94 | loop fusion | flops 1048576 | bytes 4194368 | tf_op jit(solution)/shard_map/jit(_where)/select_n | solution.py:107
  202.3 5.2 %all-to-all-start.1 = ((f32[4,8,128,128]{3,2,1,0:T(8,128)}), f32[4,8,128,128]{3,2,1,0:T(8,128)}, u32[]{:S(2)}, u32[]{:S(2)}) async-start(f32[4,8,128,128]{3,2,1,0:T(8,128)} %bitcast.8), calls=%async_computation.1 | async-start | bytes 4194304 | tf_op jit(solution)/shard_map/all_to_all | solution.py:147
  207.5 23.0 %while.85 = (s32[]{:T(128)}, f32[2048,128]{1,0:T(8,128)S(1)}, f32[]{:T(128)}, s32[4,512]{1,0:T(4,128)}, bf16[4,512,128]{2,1,0:T(8,128)(2,1)}, /*index=5*/bf16[20...) while((s32[]{:T(128)}, f32[2048,128]{1,0:T(8,128)S(1)}, f32[]{:T(128)}, ...), condition=%wide.region_22.25_spmd.clone, body=%wide.region_21.24_spmd.clone.sunk | while | flops 549193728 | bytes 2908779 | solution.py:89
  208.3 5.0 %fusion.172 = f32[2048,128]{1,0:T(8,128)S(1)} fusion(bf16[2048,128]{1,0:T(8,128)(2,1)S(1)} %get-tuple-element.1003, f32[]{:T(128)} %get-tuple-element.1004, f32[]{:T(128)} %get-tuple-element.1000, s32[2048]{0:T(1024)S(1)} %iota_add_fusion.17, s32[512]{0:T(512)S(1)} %bitcast.167, f32[2048,128]{1,0:T(8,128)S(1)} %get-tuple-element.990, ...), kind=kOutput, calls=%fused_computation.85.clone.1 | convolution fusion | flops 549191680 | bytes 2896385 | tf_op jit(solution)/shard_map/while/body/eval_jaxpr/dot_general | solution.py:82
  214.1 5.0 %fusion.172 = f32[2048,128]{1,0:T(8,128)S(1)} fusion(bf16[2048,128]{1,0:T(8,128)(2,1)S(1)} %get-tuple-element.1003, f32[]{:T(128)} %get-tuple-element.1004, f32[]{:T(128)} %get-tuple-element.1000, s32[2048]{0:T(1024)S(1)} %iota_add_fusion.17, s32[512]{0:T(512)S(1)} %bitcast.167, f32[2048,128]{1,0:T(8,128)S(1)} %get-tuple-element.990, ...), kind=kOutput, calls=%fused_computation.85.clone.1 | convolution fusion | flops 549191680 | bytes 2896385 | tf_op jit(solution)/shard_map/while/body/eval_jaxpr/dot_general | solution.py:82
  219.8 5.0 %fusion.172 = f32[2048,128]{1,0:T(8,128)S(1)} fusion(bf16[2048,128]{1,0:T(8,128)(2,1)S(1)} %get-tuple-element.1003, f32[]{:T(128)} %get-tuple-element.1004, f32[]{:T(128)} %get-tuple-element.1000, s32[2048]{0:T(1024)S(1)} %iota_add_fusion.17, s32[512]{0:T(512)S(1)} %bitcast.167, f32[2048,128]{1,0:T(8,128)S(1)} %get-tuple-element.990, ...), kind=kOutput, calls=%fused_computation.85.clone.1 | convolution fusion | flops 549191680 | bytes 2896385 | tf_op jit(solution)/shard_map/while/body/eval_jaxpr/dot_general | solution.py:82
  225.5 5.0 %fusion.172 = f32[2048,128]{1,0:T(8,128)S(1)} fusion(bf16[2048,128]{1,0:T(8,128)(2,1)S(1)} %get-tuple-element.1003, f32[]{:T(128)} %get-tuple-element.1004, f32[]{:T(128)} %get-tuple-element.1000, s32[2048]{0:T(1024)S(1)} %iota_add_fusion.17, s32[512]{0:T(512)S(1)} %bitcast.167, f32[2048,128]{1,0:T(8,128)S(1)} %get-tuple-element.990, ...), kind=kOutput, calls=%fused_computation.85.clone.1 | convolution fusion | flops 549191680 | bytes 2896385 | tf_op jit(solution)/shard_map/while/body/eval_jaxpr/dot_general | solution.py:82
  235.8 3.2 %select_select_fusion = f32[32,128,128]{2,1,0:T(8,128)} fusion(f32[32,128,128]{2,1,0:T(8,128)} %gather_fusion.3, pred[32]{0:T(512)(128)(4,1)S(1)} %copy-done.20, pred[32]{0:T(512)(128)(4,1)S(1)} %copy-done.22), kind=kLoop, calls=%fused_computation.93 | loop fusion | flops 1048576 | bytes 4194368 | tf_op jit(solution)/shard_map/jit(_where)/select_n | solution.py:107
  239.0 3.8 %all-to-all-start.3 = ((f32[4,8,128,128]{3,2,1,0:T(8,128)}), f32[4,8,128,128]{3,2,1,0:T(8,128)S(1)}, u32[]{:S(2)}, u32[]{:S(2)}) async-start(f32[4,8,128,128]{3,2,1,0:T(8,128)} %bitcast.18), calls=%async_computation.3 | async-start | bytes 4194304 | tf_op jit(solution)/shard_map/all_to_all | solution.py:149
  242.9 27.9 %scatter_custom_fusion = f32[1024,128]{1,0:T(8,128)} fusion(s32[4096]{0:T(1024)} %bitcast.3, f32[4096,128]{1,0:T(8,128)} %bitcast.9, f32[]{:T(128)} %constant.133.clone.1), kind=kCustom, calls=%fused_computation.99 | custom fusion | flops 524288 | bytes 524800 | tf_op jit(solution)/shard_map/scatter-add | solution.py:152
  270.8 27.8 %scatter_custom_fusion.1 = f32[1024,128]{1,0:T(8,128)} fusion(s32[4096]{0:T(1024)S(1)} %bitcast.172, f32[4096,128]{1,0:T(8,128)S(1)} %bitcast.163, f32[]{:T(128)} %constant.133.clone.1), kind=kCustom, calls=%fused_computation.97 | custom fusion | flops 524288 | bytes 524292 | tf_op jit(solution)/shard_map/scatter-add | solution.py:155
  (169 shorter events, 49.0 us)
Async XLA Ops:
  0.6 4.9 %copy-start = (s32[2048]{0:T(1024)S(1)}, s32[2048]{0:T(1024)}, u32[]{:S(2)}) copy-start(s32[2048]{0:T(1024)} %param.32) | copy-start | bytes 24580
  0.6 99.4 %collective-permute-start = (bf16[2048,128]{1,0:T(8,128)(2,1)}, bf16[2048,128]{1,0:T(8,128)(2,1)}, u32[]{:S(2)}, u32[]{:S(2)}) collective-permute-start(bf16[2048,128]{1,0:T(8,128)(2,1)} %param.28), channel_id=1, source_target_pairs={{124,0},{0,4},{4,8},{8,12},{12,16},{16,20},{20,24},{24,28},{28,32}... | collective-permute-start | bytes 1572872 | tf_op jit(solution)/shard_map/ppermute | solution.py:15
  5.4 16.1 %copy-start.15 = (pred[32]{0:T(512)(128)(4,1)}, pred[32]{0:T(512)(128)(4,1)S(1)}, u32[]{:S(2)}) copy-start(pred[32]{0:T(512)(128)(4,1)S(1)} %compare_and_fusion.1) | copy-start | bytes 100
  5.5 16.0 %copy-start.17 = (pred[32]{0:T(512)(128)(4,1)}, pred[32]{0:T(512)(128)(4,1)S(1)}, u32[]{:S(2)}) copy-start(pred[32]{0:T(512)(128)(4,1)S(1)} %fusion.94) | copy-start | bytes 100
  5.6 16.0 %copy-start.13 = (s32[1024]{0:T(1024)}, s32[1024]{0:T(1024)S(1)}, u32[]{:S(2)}) copy-start(s32[1024]{0:T(1024)S(1)} %pad_clamp_fusion.1) | copy-start | bytes 12292
  6.8 184.6 %all-to-all-start = ((s32[4,8,128]{2,1,0:T(8,128)}), s32[4,8,128]{2,1,0:T(8,128)}, u32[]{:S(2)}, u32[]{:S(2)}) async-start(s32[4,8,128]{2,1,0:T(8,128)} %fusion.91), calls=%async_computation | async-start | bytes 32768 | tf_op jit(solution)/shard_map/all_to_all | solution.py:148
  12.6 59.1 %collective-permute-start.4 = (bf16[2048,128]{1,0:T(8,128)(2,1)}, bf16[2048,128]{1,0:T(8,128)(2,1)}, u32[]{:S(2)}, u32[]{:S(2)}) collective-permute-start(bf16[2048,128]{1,0:T(8,128)(2,1)} %param.27), channel_id=1, source_target_pairs={{4,0},{8,4},{12,8},{16,12},{20,16},{24,20},{28,24},{32,28},{36,32}... | collective-permute-start | bytes 1572872 | tf_op jit(solution)/shard_map/ppermute | solution.py:15
  17.7 43.8 %collective-permute-start.3 = (s32[2048]{0:T(1024)}, s32[2048]{0:T(1024)S(1)}, u32[]{:S(2)}, u32[]{:S(2)}) collective-permute-start(s32[2048]{0:T(1024)} %param.31), channel_id=1, source_target_pairs={{4,0},{8,4},{12,8},{16,12},{20,16},{24,20},{28,24},{32,28},{36,32}... | collective-permute-start | bytes 24584 | tf_op jit(solution)/shard_map/ppermute | solution.py:15
  23.3 37.1 %copy-start.23 = (s32[16,1]{0,1:T(1,128)S(1)}, s32[16,1]{0,1:T(1,128)}, u32[]{:S(2)}) copy-start(s32[16,1]{0,1:T(1,128)} %param.35) | copy-start | bytes 196
  23.3 38.8 %copy-start.6 = (s32[2048]{0:T(1024)S(1)}, s32[2048]{0:T(1024)}, u32[]{:S(2)}) copy-start(s32[2048]{0:T(1024)} %param.33) | copy-start | bytes 24580
  27.8 2.8 copy-start.3
  37.1 2.8 copy-start.3
  46.4 2.8 copy-start.3
  55.6 2.8 copy-start.3
  60.5 11.3 %copy-start.1 = (f32[2048,128]{1,0:T(8,128)}, f32[2048,128]{1,0:T(8,128)S(1)}, u32[]{:S(2)}) copy-start(f32[2048,128]{1,0:T(8,128)S(1)} %get-tuple-element.312) | copy-start | bytes 3145732
  61.4 10.3 %copy-start.19 = (pred[32]{0:T(512)(128)(4,1)}, pred[32]{0:T(512)(128)(4,1)S(1)}, u32[]{:S(2)}) copy-start(pred[32]{0:T(512)(128)(4,1)S(1)} %compare_and_fusion) | copy-start | bytes 100
  61.5 10.2 %copy-start.21 = (pred[32]{0:T(512)(128)(4,1)}, pred[32]{0:T(512)(128)(4,1)S(1)}, u32[]{:S(2)}) copy-start(pred[32]{0:T(512)(128)(4,1)S(1)} %fusion.92) | copy-start | bytes 100
  61.5 4.1 %collective-permute-start.5 = (s32[2048]{0:T(1024)S(1)}, s32[2048]{0:T(1024)S(1)}, u32[]{:S(2)}, u32[]{:S(2)}) collective-permute-start(s32[2048]{0:T(1024)S(1)} %collective-permute-done.3), channel_id=1, source_target_pairs={{4,0},{8,4},{12,8},{16,12},{20,16},{24,20},{28,24},{32,28},{36,32}... | collective-permute-start | bytes 24584 | tf_op jit(solution)/shard_map/ppermute | solution.py:15
  62.1 0.6 copy-start.14
  65.6 5.5 %collective-permute-start.7 = (s32[2048]{0:T(1024)S(1)}, s32[2048]{0:T(1024)S(1)}, u32[]{:S(2)}, u32[]{:S(2)}) collective-permute-start(s32[2048]{0:T(1024)S(1)} %collective-permute-done.5), channel_id=1, source_target_pairs={{4,0},{8,4},{12,8},{16,12},{20,16},{24,20},{28,24},{32,28},{36,32}... | collective-permute-start | bytes 24584 | tf_op jit(solution)/shard_map/ppermute | solution.py:15
  71.7 28.3 %copy-start.12 = (bf16[4,512,128]{2,1,0:T(8,128)(2,1)S(1)}, bf16[4,512,128]{2,1,0:T(8,128)(2,1)}, u32[]{:S(2)}) copy-start(bf16[4,512,128]{2,1,0:T(8,128)(2,1)} %get-tuple-element.1067) | copy-start | bytes 1572868
  92.5 7.5 %copy-start.11 = (f32[2048,128]{1,0:T(8,128)}, f32[2048,128]{1,0:T(8,128)S(1)}, u32[]{:S(2)}) copy-start(f32[2048,128]{1,0:T(8,128)S(1)} %get-tuple-element.313) | copy-start | bytes 3145732
  92.5 26.1 %collective-permute-start.6 = (bf16[2048,128]{1,0:T(8,128)(2,1)}, bf16[2048,128]{1,0:T(8,128)(2,1)}, u32[]{:S(2)}, u32[]{:S(2)}) collective-permute-start(bf16[2048,128]{1,0:T(8,128)(2,1)} %collective-permute-done.4), channel_id=1, source_target_pairs={{4,0},{8,4},{12,8},{16,12},{20,16},{24,20},{28,24},{32,28},{36,32}... | collective-permute-start | bytes 1572872 | tf_op jit(solution)/shard_map/ppermute | solution.py:15
  100.1 18.5 %copy-start.4 = (bf16[2048,128]{1,0:T(8,128)(2,1)S(1)}, bf16[2048,128]{1,0:T(8,128)(2,1)}, u32[]{:S(2)}) copy-start(bf16[2048,128]{1,0:T(8,128)(2,1)} %get-tuple-element.1063) | copy-start | bytes 1572868
  100.1 18.5 %copy-start.9 = (f32[2048,128]{1,0:T(8,128)S(1)}, f32[2048,128]{1,0:T(8,128)}, u32[]{:S(2)}) copy-start(f32[2048,128]{1,0:T(8,128)} %custom-call.2) | copy-start | bytes 3145732
  118.3 20.4 %collective-permute-start.1 = (bf16[2048,128]{1,0:T(8,128)(2,1)}, bf16[2048,128]{1,0:T(8,128)(2,1)}, u32[]{:S(2)}, u32[]{:S(2)}) collective-permute-start(bf16[2048,128]{1,0:T(8,128)(2,1)} %collective-permute-done), channel_id=1, source_target_pairs={{124,0},{0,4},{4,8},{8,12},{12,16},{16,20},{20,24},{24,28},{28,32}... | collective-permute-start | bytes 1572872 | tf_op jit(solution)/shard_map/ppermute | solution.py:15
  138.8 1.0 copy-start.10
  139.8 25.5 %collective-permute-start.2 = (bf16[2048,128]{1,0:T(8,128)(2,1)}, bf16[2048,128]{1,0:T(8,128)(2,1)}, u32[]{:S(2)}, u32[]{:S(2)}) collective-permute-start(bf16[2048,128]{1,0:T(8,128)(2,1)} %collective-permute-done.1), channel_id=1, source_target_pairs={{124,0},{0,4},{4,8},{8,12},{12,16},{16,20},{20,24},{24,28},{28,32}... | collective-permute-start | bytes 1572872 | tf_op jit(solution)/shard_map/ppermute | solution.py:15
  158.0 8.4 %copy-start.5 = (f32[4,512,128]{2,1,0:T(8,128)}, f32[4,512,128]{2,1,0:T(8,128)S(1)}, u32[]{:S(2)}) copy-start(f32[4,512,128]{2,1,0:T(8,128)S(1)} %get-tuple-element.309) | copy-start | bytes 3145732
  158.0 49.5 %collective-permute-start.8 = (bf16[2048,128]{1,0:T(8,128)(2,1)}, bf16[2048,128]{1,0:T(8,128)(2,1)}, u32[]{:S(2)}, u32[]{:S(2)}) collective-permute-start(bf16[2048,128]{1,0:T(8,128)(2,1)} %collective-permute-done.6), channel_id=1, source_target_pairs={{4,0},{8,4},{12,8},{16,12},{20,16},{24,20},{28,24},{32,28},{36,32}... | collective-permute-start | bytes 1572872 | tf_op jit(solution)/shard_map/ppermute | solution.py:15
  189.3 9.8 %copy-start.16 = (pred[32]{0:T(512)(128)(4,1)S(1)}, pred[32]{0:T(512)(128)(4,1)}, u32[]{:S(2)}) copy-start(pred[32]{0:T(512)(128)(4,1)} %copy-done.15) | copy-start | bytes 100
  189.4 9.8 %copy-start.18 = (pred[32]{0:T(512)(128)(4,1)S(1)}, pred[32]{0:T(512)(128)(4,1)}, u32[]{:S(2)}) copy-start(pred[32]{0:T(512)(128)(4,1)} %copy-done.17) | copy-start | bytes 100
  191.5 10.8 %all-to-all-start.2 = ((s32[4,8,128]{2,1,0:T(8,128)}), s32[4,8,128]{2,1,0:T(8,128)S(1)}, u32[]{:S(2)}, u32[]{:S(2)}) async-start(s32[4,8,128]{2,1,0:T(8,128)} %fusion.90), calls=%async_computation.2 | async-start | bytes 32768 | tf_op jit(solution)/shard_map/all_to_all | solution.py:150
  202.3 5.2 %copy-start.7 = (f32[2048,128]{1,0:T(8,128)S(1)}, f32[2048,128]{1,0:T(8,128)}, u32[]{:S(2)}) copy-start(f32[2048,128]{1,0:T(8,128)} %custom-call.3) | copy-start | bytes 3145732
  202.3 36.7 %all-to-all-start.1 = ((f32[4,8,128,128]{3,2,1,0:T(8,128)}), f32[4,8,128,128]{3,2,1,0:T(8,128)}, u32[]{:S(2)}, u32[]{:S(2)}) async-start(f32[4,8,128,128]{3,2,1,0:T(8,128)} %bitcast.8), calls=%async_computation.1 | async-start | bytes 4194304 | tf_op jit(solution)/shard_map/all_to_all | solution.py:147
  207.5 24.0 %copy-start.2 = (f32[2048,128]{1,0:T(8,128)S(1)}, f32[2048,128]{1,0:T(8,128)}, u32[]{:S(2)}) copy-start(f32[2048,128]{1,0:T(8,128)} %copy-done.1) | copy-start | bytes 3145732
  230.5 1.0 copy-start.8
  233.7 2.1 copy-start.20
  233.7 2.1 copy-start.22
  239.0 31.7 %all-to-all-start.3 = ((f32[4,8,128,128]{3,2,1,0:T(8,128)}), f32[4,8,128,128]{3,2,1,0:T(8,128)S(1)}, u32[]{:S(2)}, u32[]{:S(2)}) async-start(f32[4,8,128,128]{3,2,1,0:T(8,128)} %bitcast.18), calls=%async_computation.3 | async-start | bytes 4194304 | tf_op jit(solution)/shard_map/all_to_all | solution.py:149
where the time goes:
time: 300 us; the launch traced here: 299 us
  matrix products  154 us (51%)
  other arithmetic  71.9 us (24%)
  starting transfers between devices  53.6 us (18%)
  local copies, waits for them, and re-layouts  14.2 us (5%)
  waiting for transfers between devices  3.01 us (1%)
    dot_general x12, matrix products, merchant_one_block(): lax.dot_general(delta, piece, (((0,), (0,)), ((), ())), preferred_element...  60.3 us
    dot_general x12, matrix products, account_one_block(): jnp.dot(delta, merch_block, preferred_element_type=jnp.float32)  56.7 us
    ppermute x9, starting transfers between devices, shifted(): return lax.ppermute(block, axis, route)  31.2 us
    scatter-add x1, other arithmetic, per_device(): jax.ops.segment_sum(acc_payload.reshape(-1, D), acc_keys.reshape(-1), num...  27.9 us
    scatter-add x1, other arithmetic, per_device(): jax.ops.segment_sum(merch_payload.reshape(-1, D), merch_keys.reshape(-1),...  27.8 us
    dot_general x4, matrix products, score_delta(): lax.dot_general(piece, merch_block, (((1,), (1,)), ((), ())), preferred_e...  17.7 us
    dot_general x4, matrix products, tile_one_block(): lax.dot_general(delta, piece, (((0,), (0,)), ((), ())), preferred_element...  10.9 us
    dot_general x4, matrix products, tile_one_block(): jnp.dot(delta, merch_block, preferred_element_type=jnp.float32)  8.3 us
  transfers between devices with their start and end apart: 13, of which 2 were waited for; matrix products, arithmetic and copies ran while one was open for 70% of the time, Pallas kernels for 0%

commit v1 on v0

v1 whole, which is shorter than its diff:
```python
import functools

import jax
import jax.numpy as jnp
from jax import lax
from jax.experimental import pallas as pl
from jax.experimental.pallas import tpu as pltpu
from jax.sharding import PartitionSpec as P

D = 128
BLOCK_ROWS = 128
TROWS = 1024
N = 2048
BLOCKS = N // BLOCK_ROWS
TILE = 256
NT = (((1,), (1,)), ((), ()))
BASE = 64


def shifted(block, distance):
    devices = range(lax.axis_size("blk"))
    route = [((i - distance) % len(devices), i) for i in devices]
    return lax.ppermute(block, "blk", route)


def tab_swap(block, bit):
    return lax.ppermute(block, "tab", [(k, k ^ bit) for k in range(4)])


def one_pass(x, y, left, right, out, half_scale, half_bias):
    for c in range(0, N, TILE):
        cols = y[c : c + TILE, :]
        logits = lax.dot_general(x[...], cols, NT, preferred_element_type=jnp.float32)
        t = jnp.tanh(logits * half_scale + half_bias)
        parts = []
        for k in range(0, TILE, 128):
            j = (c + k) // 128
            hit = left[...] == right[j : j + 1, :]
            parts.append(t[:, k : k + 128] + jnp.where(hit, jnp.float32(-1), jnp.float32(1)))
        delta2 = jnp.concatenate(parts, axis=1).astype(jnp.bfloat16)
        out[...] += jnp.dot(delta2, cols, preferred_element_type=jnp.float32)


def lane_iota():
    shape = (BLOCKS, 128)
    return lax.broadcasted_iota(jnp.int32, shape, 0) * 128 + lax.broadcasted_iota(jnp.int32, shape, 1)


def row_iota():
    return lax.broadcasted_iota(jnp.int32, (N, 128), 0)


def guest_labels(guest, step):
    high = guest[N : N + BLOCKS, :].astype(jnp.float32)
    low = guest[N + BLOCKS : N + 2 * BLOCKS, :].astype(jnp.float32)
    return (high * BASE + low).astype(jnp.int32) - step * N


def both_passes(xs, ys, left, right, out, half_scale, half_bias):
    def body(p, carry):
        one_pass(xs.at[p], ys.at[p], left.at[p], right.at[p], out.at[p], half_scale, half_bias)
        return carry

    lax.fori_loop(0, 2, body, 0)


def own_kernel(coef, acc, merch, labels, out, label_rows, xs, ys, left, right):
    for j in range(BLOCKS):
        block = jnp.broadcast_to(labels[j : j + 1, :], (128, 128))
        label_rows[j * 128 : (j + 1) * 128, :] = block.T
    xs[0] = acc[...]
    ys[0] = merch[...]
    xs[1] = merch[...]
    ys[1] = acc[...]
    left[0] = label_rows[...]
    left[1] = row_iota()
    right[0] = lane_iota()
    right[1] = labels[...]
    out[...] = jnp.zeros_like(out)
    both_passes(xs, ys, left, right, out, coef[0], coef[1])


def step_kernel(coef, acc, merch, visiting, guest, label_rows, prev, out, xs, ys, left, right, *, step):
    xs[0] = acc[...]
    ys[0] = visiting[...]
    xs[1] = merch[...]
    ys[1] = guest[0:N, :]
    left[0] = label_rows[...] - step * N
    left[1] = row_iota()
    right[0] = lane_iota()
    right[1] = guest_labels(guest, step)
    out[...] = prev[...]
    both_passes(xs, ys, left, right, out, coef[0], coef[1])


def scatter_blocks(grad, scale, ids, owner, here, table, keep, send):
    table[...] = jnp.zeros_like(table)
    target_rows = lax.broadcasted_iota(jnp.int32, (TROWS, 128), 0)

    def body(j, carry):
        first = pl.multiple_of(j * BLOCK_ROWS, BLOCK_ROWS)
        rows = grad[pl.ds(first, BLOCK_ROWS), :] * scale
        high = rows.astype(jnp.bfloat16)
        low = (rows - high.astype(jnp.float32)).astype(jnp.bfloat16)
        pair = jnp.concatenate([high, low], axis=1)
        hot = jnp.where(target_rows == ids[pl.ds(j, 1), :], jnp.float32(1), jnp.float32(0)).astype(jnp.bfloat16)
        both = jnp.dot(hot, pair, preferred_element_type=jnp.float32)
        slot = (owner[j] ^ here) & 3
        place = pl.multiple_of((slot // 2 + (slot % 2) * 2) * TROWS, TROWS)
        table[pl.ds(place, TROWS), :] += both[:, :D] + both[:, D:]
        return carry

    lax.fori_loop(0, BLOCKS, body, 0, unroll=4)
    keep[...] = table[0 : 2 * TROWS, :].reshape(2, TROWS, D)
    send[...] = table[2 * TROWS : 4 * TROWS, :].reshape(2, TROWS, D)


def last_account_kernel(coef, owner, here, acc, visiting, label_rows, prev, ids, keep, send, out, left, right, table):
    left[...] = label_rows[...] - 3 * N
    right[...] = lane_iota()
    out[...] = prev[0]
    one_pass(acc, visiting, left, right, out, coef[0], coef[1])
    scatter_blocks(out, coef[0], ids, owner, here[0], table, keep, send)


def last_merchant_kernel(coef, owner, here, merch, guest, prev, ids, keep, send, out, left, right, table):
    left[...] = row_iota()
    right[...] = guest_labels(guest, 3)
    out[...] = prev[1]
    one_pass(merch, guest, left, right, out, coef[0], coef[1])
    scatter_blocks(out, coef[0], ids, owner, here[0], table, keep, send)


def call(kernel, smem, vmem, out_shape, scratch, flops, alias=None):
    in_specs = [pl.BlockSpec(memory_space=pltpu.SMEM)] * smem + [pl.BlockSpec(memory_space=pltpu.VMEM)] * vmem
    out_specs = jax.tree.map(lambda _: pl.BlockSpec(memory_space=pltpu.VMEM), out_shape)
    return pl.pallas_call(
        kernel,
        in_specs=in_specs,
        out_specs=out_specs,
        out_shape=out_shape,
        scratch_shapes=scratch,
        input_output_aliases=alias or {},
        cost_estimate=pl.CostEstimate(flops=flops, bytes_accessed=4 << 20, transcendentals=0),
        compiler_params=pltpu.CompilerParams(vmem_limit_bytes=36 << 20),
    )


GRADS = pltpu.VMEM((2, N, D), jnp.float32)
LABELS = pltpu.VMEM((N, 128), jnp.int32)
TABLES = jax.ShapeDtypeStruct((2, TROWS, D), jnp.float32)
PAIR_SCRATCH = [
    pltpu.VMEM((2, N, D), jnp.bfloat16),
    pltpu.VMEM((2, N, D), jnp.bfloat16),
    pltpu.VMEM((2, N, 128), jnp.int32),
    pltpu.VMEM((2, BLOCKS, 128), jnp.int32),
]
LAST_SCRATCH = [
    pltpu.VMEM((N, D), jnp.float32),
    pltpu.VMEM((N, 128), jnp.int32),
    pltpu.VMEM((BLOCKS, 128), jnp.int32),
    pltpu.VMEM((4 * TROWS, D), jnp.float32),
]


PASS = 3 << 30


def in_vmem(block):
    return pltpu.with_memory_space_constraint(block, pltpu.VMEM)


def exchange(keep, send):
    both = keep + tab_swap(send, 1)
    return both[0] + tab_swap(both[1], 2)


def per_device(
    accounts,
    merchants,
    logit_scale,
    logit_bias,
    positive,
    account_ids,
    merchant_ids,
    account_owner,
    merchant_owner,
):
    coef = 0.5 * jnp.concatenate([logit_scale, logit_bias])
    here = lax.axis_index("tab").astype(jnp.int32).reshape(1)
    labels = positive.reshape(BLOCKS, 128)
    digits = jnp.concatenate([labels // BASE, labels % BASE], axis=0).astype(jnp.bfloat16)
    guests = jnp.concatenate([accounts, digits], axis=0)

    visiting2 = shifted(merchants, 2)
    visiting1 = shifted(merchants, 1)
    guest2 = shifted(guests, -2)
    guest1 = shifted(guests, -1)

    grads, label_rows = call(own_kernel, 1, 3, [GRADS, LABELS], PAIR_SCRATCH, 2 * PASS)(
        coef, accounts, merchants, labels
    )
    grads = call(functools.partial(step_kernel, step=2), 1, 6, GRADS, PAIR_SCRATCH, 2 * PASS, {6: 0})(
        coef, accounts, merchants, visiting2, guest2, in_vmem(label_rows), in_vmem(grads)
    )
    visiting1, guest1, grads = lax.optimization_barrier((visiting1, guest1, grads))
    visiting3 = shifted(visiting1, 2)
    guest3 = shifted(guest1, -2)
    grads = call(functools.partial(step_kernel, step=1), 1, 6, GRADS, PAIR_SCRATCH, 2 * PASS, {6: 0})(
        coef, accounts, merchants, visiting1, guest1, in_vmem(label_rows), in_vmem(grads)
    )
    visiting3, guest3, grads = lax.optimization_barrier((visiting3, guest3, grads))
    keep, send = call(last_account_kernel, 3, 5, [TABLES, TABLES], LAST_SCRATCH, 2 * PASS)(
        coef, account_owner[:, 0], here, accounts, visiting3, in_vmem(label_rows), in_vmem(grads), account_ids.reshape(BLOCKS, 128)
    )
    account_grad = exchange(keep, send)
    keep, send = call(last_merchant_kernel, 3, 4, [TABLES, TABLES], LAST_SCRATCH, 2 * PASS)(
        coef, merchant_owner[:, 0], here, merchants, guest3, in_vmem(grads), merchant_ids.reshape(BLOCKS, 128)
    )
    merchant_grad = exchange(keep, send)
    return (account_grad, merchant_grad)


def solution(mesh):
    return jax.shard_map(
        per_device,
        mesh=mesh,
        in_specs=(
            P(("blk", "tab"), None),
            P(("blk", "tab"), None),
            P(),
            P(),
            P(("blk", "tab")),
            P(("blk", "tab")),
            P(("blk", "tab")),
            P(("blk", "tab"), None),
            P(("blk", "tab"), None),
        ),
        out_specs=(P(("blk", "tab"), None), P(("blk", "tab"), None)),
        check_vma=False,
    )
```

time: 300 us -> 112 us (0.37)
  matrix products: 154 us -> 0 us
  other arithmetic: 71.9 us -> 4.68 us
  Pallas kernels: 0 us -> 48.9 us
  starting transfers between devices: 53.6 us -> 16.6 us
  waiting for transfers between devices: 3.01 us -> 37.4 us
  local copies, waits for them, and re-layouts: 14.2 us -> 0.11 us
    dot_general x36 -> x0, matrix products: 154 us -> none  [the longest x12 60.3 us: merchant_one_block(): lax.dot_general(delta, piece, (((0,), (0,)), ((), ())), preferred_element...]
    scatter-add x2 -> x0, other arithmetic: 55.7 us -> none  [the longest x1 27.9 us: per_device(): jax.ops.segment_sum(acc_payload.reshape(-1, D), acc_keys.reshape(-1), num...]
    pallas_call x0 -> x5, Pallas kernels: none -> 48.9 us  [the longest x1 10.6 us: per_device(): call(own_kernel, 1, 3, [GRADS, LABELS], PAIR_SCRATCH, 2 * PASS)]
    ppermute x9 -> x10, waiting for transfers between devices: 3 us -> 37.4 us  [the longest x4 20.8 us: tab_swap(): return lax.ppermute(block, 'tab', [(k, k ^ bit) for k in range(4)])]
    all_to_all x4 -> x0, starting transfers between devices: 22.5 us -> none  [the longest x1 7.65 us: per_device(): lax.all_to_all(merch_keys, 'tab', split_axis=0, concat_axis=0, tiled=True)]
    ppermute x9 -> x10, starting transfers between devices: 31.2 us -> 16.6 us  [the longest x6 10.8 us: shifted(): return lax.ppermute(block, 'blk', route)]
    select_n x4 -> x0, other arithmetic: 6.4 us -> none  [the longest x2 6.4 us: pack_blocks(): payload = jnp.where(filled[:, None, None], payload, jnp.float32(0.0))]
    gather x4 -> x0, local copies, waits for them, and re-layouts: 5.38 us -> none  [the longest x2 4.23 us: pack_blocks(): jnp.take(grads.reshape(block_count, BLOCK_ROWS, D), source, axis=0)]
  transfers between devices with their start and end apart: 13 -> 10, of which waited for: 2 -> 5; matrix products, arithmetic and copies ran while one was open for 70% -> 1% of each run, Pallas kernels for 0% -> 37%
where the time goes in v1:
time: 112 us; the launch traced here: 110 us
  Pallas kernels  48.9 us (44%)
  waiting for transfers between devices  37.4 us (33%)
  starting transfers between devices  16.6 us (15%)
  other arithmetic  4.68 us (4%)
  between operations  2.08 us (2%)
    ppermute x4, waiting for transfers between devices, tab_swap(): return lax.ppermute(block, 'tab', [(k, k ^ bit) for k in range(4)])  20.8 us
    ppermute x6, waiting for transfers between devices, shifted(): return lax.ppermute(block, 'blk', route)  16.6 us
    ppermute x6, starting transfers between devices, shifted(): return lax.ppermute(block, 'blk', route)  10.8 us
    pallas_call x1, Pallas kernels, per_device(): call(own_kernel, 1, 3, [GRADS, LABELS], PAIR_SCRATCH, 2 * PASS)  10.6 us
    pallas_call x1, Pallas kernels, per_device(): call(functools.partial(step_kernel, step=2), 1, 6, GRADS, PAIR_SCRATCH, 2...  10.4 us
    pallas_call x1, Pallas kernels, per_device(): call(functools.partial(step_kernel, step=1), 1, 6, GRADS, PAIR_SCRATCH, 2...  10.4 us
    pallas_call x1, Pallas kernels, per_device(): call(last_account_kernel, 3, 5, [TABLES, TABLES], LAST_SCRATCH, 2 * PASS)  8.79 us
    pallas_call x1, Pallas kernels, per_device(): call(last_merchant_kernel, 3, 4, [TABLES, TABLES], LAST_SCRATCH, 2 * PASS)  8.7 us
  transfers between devices with their start and end apart: 10, of which 5 were waited for; matrix products, arithmetic and copies ran while one was open for 1% of the time, Pallas kernels for 37%

profile of v1, /device:TPU:3, one launch (start us, length us, event | category | flops | bytes accessed | tf_op | source)
XLA Modules:
  0.0 109.8 jit_solution(10233273174116460669)
XLA Ops:
  0.6 0.0 copy-start.1
  0.6 0.0 copy-start
  0.7 0.0 copy-start.2
  0.7 0.8 fusion.2
  1.5 1.9 %pad_maximum_fusion = bf16[2080,128]{1,0:T(8,128)(2,1)} fusion(bf16[16,128]{1,0:T(8,128)(2,1)S(1)} %get-tuple-element.27, bf16[16,128]{1,0:T(8,128)(2,1)S(1)} %get-tuple-element.26, bf16[2048,128]{1,0:T(8,128)(2,1)} %acc.7), kind=kLoop, calls=%fused_computation | loop fusion | flops 1597440 | bytes 1064960 | tf_op jit(solution)/shard_map/concatenate | solution.py:193
  3.3 6.2 %collective-permute-start.3 = (bf16[2080,128]{1,0:T(8,128)(2,1)}, bf16[2080,128]{1,0:T(8,128)(2,1)S(1)}, u32[]{:S(2)}, u32[]{:S(2)}) collective-permute-start(bf16[2080,128]{1,0:T(8,128)(2,1)} %pad_maximum_fusion), channel_id=1, source_target_pairs={{8,0},{12,4},{16,8},{20,12},{24,16},{28,20},{32,24},{36,28},{40,32... | collective-permute-start | bytes 1597448 | tf_op jit(solution)/shard_map/ppermute | solution.py:23
  9.5 1.7 %collective-permute-start.1 = (bf16[2080,128]{1,0:T(8,128)(2,1)}, bf16[2080,128]{1,0:T(8,128)(2,1)S(1)}, u32[]{:S(2)}, u32[]{:S(2)}) collective-permute-start(bf16[2080,128]{1,0:T(8,128)(2,1)} %pad_maximum_fusion), channel_id=1, source_target_pairs={{4,0},{8,4},{12,8},{16,12},{20,16},{24,20},{28,24},{32,28},{36,32}... | collective-permute-start | bytes 1597448 | tf_op jit(solution)/shard_map/ppermute | solution.py:23
  11.2 0.0 copy-done.2
  11.2 1.3 %collective-permute-start.2 = (bf16[2048,128]{1,0:T(8,128)(2,1)S(1)}, bf16[2048,128]{1,0:T(8,128)(2,1)S(1)}, u32[]{:S(2)}, u32[]{:S(2)}) collective-permute-start(bf16[2048,128]{1,0:T(8,128)(2,1)S(1)} %copy-done.2), channel_id=1, source_target_pairs={{120,0},{124,4},{0,8},{4,12},{8,16},{12,20},{16,24},{20,28},{24,32... | collective-permute-start | bytes 1572872 | tf_op jit(solution)/shard_map/ppermute | solution.py:23
  12.6 0.0 collective-permute-start
  13.9 0.1 maximum_multiply_fusion.coef
  14.0 0.0 copy-done.1
  14.0 0.0 copy-done
  14.0 10.6 %shard_map.104 = (f32[2,2048,128]{2,1,0:T(8,128)S(1)}, s32[2048,128]{1,0:T(8,128)S(1)}) custom-call(f32[2]{0:T(128)S(1)} %maximum_multiply_fusion.coef, bf16[2048,128]{1,0:T(8,128)(2,1)S(1)} %copy-done, bf16[2048,128]{1,0:T(8,128)(2,1)S(1)} %copy-done.2, s32[16,128]{1,0:T(8,128)S(1)} %bitcast.20), custom_call_target="tpu_custom_call" | custom-call | flops 6442450944 | bytes 4194304 | tf_op jit(solution)/shard_map/pallas_call | solution.py:200
  24.5 13.5 %collective-permute-done.2.visiting = bf16[2048,128]{1,0:T(8,128)(2,1)S(1)} collective-permute-done((bf16[2048,128]{1,0:T(8,128)(2,1)S(1)}, bf16[2048,128]{1,0:T(8,128)(2,1)S(1)}, u32[]{:S(2)}, u32[]{:S(2)}) %collective-permute-start.2) | collective-permute-done | bytes 524320 | tf_op jit(solution)/shard_map/ppermute | solution.py:23
  38.0 0.0 collective-permute-done.3.guest
  38.0 10.4 %shard_map.105.prev = f32[2,2048,128]{2,1,0:T(8,128)S(1)} custom-call(f32[2]{0:T(128)S(1)} %maximum_multiply_fusion.coef, bf16[2048,128]{1,0:T(8,128)(2,1)S(1)} %copy-done, bf16[2048,128]{1,0:T(8,128)(2,1)S(1)} %copy-done.2, bf16[2048,128]{1,0:T(8,128)(2,1)S(1)} %collective-permute-done.2.visiting, ...), custom_call_target="tpu_custom_call", output_to_operand_aliasing={{}: (6, {})} | custom-call | flops 6442450944 | bytes 4194304 | tf_op jit(solution)/shard_map/pallas_call | solution.py:203
  48.5 0.0 copy-start.3
  48.5 0.0 copy-start.5
  48.5 0.0 collective-permute-done.visiting
  48.5 0.0 collective-permute-done.1.guest
  48.5 0.1 collective-permute-start.5
  48.6 1.5 %collective-permute-start.4 = (bf16[2048,128]{1,0:T(8,128)(2,1)S(1)}, bf16[2048,128]{1,0:T(8,128)(2,1)S(1)}, u32[]{:S(2)}, u32[]{:S(2)}) collective-permute-start(bf16[2048,128]{1,0:T(8,128)(2,1)S(1)} %collective-permute-done.visiting), channel_id=1, source_target_pairs={{120,0},{124,4},{0,8},{4,12},{8,16},{12,20},{16,24},{20,28},{24,32... | collective-permute-start | bytes 1572872 | tf_op jit(solution)/shard_map/ppermute | solution.py:23
  50.1 10.4 %shard_map.106.prev = f32[2,2048,128]{2,1,0:T(8,128)S(1)} custom-call(f32[2]{0:T(128)S(1)} %maximum_multiply_fusion.coef, bf16[2048,128]{1,0:T(8,128)(2,1)S(1)} %copy-done, bf16[2048,128]{1,0:T(8,128)(2,1)S(1)} %copy-done.2, bf16[2048,128]{1,0:T(8,128)(2,1)S(1)} %collective-permute-done.visiting, ...), custom_call_target="tpu_custom_call", output_to_operand_aliasing={{}: (6, {})} | custom-call | flops 6442450944 | bytes 4194304 | tf_op jit(solution)/shard_map/pallas_call | solution.py:209
  60.5 3.1 %collective-permute-done.4.visiting = bf16[2048,128]{1,0:T(8,128)(2,1)S(1)} collective-permute-done((bf16[2048,128]{1,0:T(8,128)(2,1)S(1)}, bf16[2048,128]{1,0:T(8,128)(2,1)S(1)}, u32[]{:S(2)}, u32[]{:S(2)}) %collective-permute-start.4) | collective-permute-done | bytes 524320 | tf_op jit(solution)/shard_map/ppermute | solution.py:23
  63.6 0.0 collective-permute-done.5.guest
  63.6 0.0 copy-done.3
  63.6 0.0 copy-done.5
  63.6 0.0 copy-start.4
  63.6 0.0 copy-start.6
  63.6 8.7 %shard_map.108 = (f32[2,1024,128]{2,1,0:T(8,128)S(1)}, f32[2,1024,128]{2,1,0:T(8,128)S(1)}) custom-call(f32[2]{0:T(128)S(1)} %maximum_multiply_fusion.coef, s32[16]{0:T(128)S(1)} %bitcast.23, s32[1]{0:T(128)} %bitcast.1.here, bf16[2048,128]{1,0:T(8,128)(2,1)S(1)} %copy-done.2, bf16[2080,128]{1,0:T(8,128)(2,1)S(1)} %collective-permute-done.5.guest, ...), custom_call_target="tpu_custom_call" | custom-call | flops 6442450944 | bytes 4194304 | tf_op jit(solution)/shard_map/pallas_call | solution.py:217
  72.3 3.3 %collective-permute-start.8 = (f32[2,1024,128]{2,1,0:T(8,128)S(1)}, f32[2,1024,128]{2,1,0:T(8,128)S(1)}, u32[]{:S(2)}, u32[]{:S(2)}) collective-permute-start(f32[2,1024,128]{2,1,0:T(8,128)S(1)} %get-tuple-element.25), channel_id=1, source_target_pairs={{0,1},{1,0},{2,3},{3,2},{4,5},{5,4},{6,7},{7,6},{8,9},{9,8},{10,11... | collective-permute-start | bytes 3145736 | tf_op jit(solution)/shard_map/ppermute | solution.py:27
  75.6 0.0 copy-done.4
  75.6 0.0 copy-done.6
  75.6 8.8 %shard_map.107 = (f32[2,1024,128]{2,1,0:T(8,128)S(1)}, f32[2,1024,128]{2,1,0:T(8,128)S(1)}) custom-call(f32[2]{0:T(128)S(1)} %maximum_multiply_fusion.coef, s32[16]{0:T(128)S(1)} %bitcast.24, s32[1]{0:T(128)} %bitcast.1.here, bf16[2048,128]{1,0:T(8,128)(2,1)S(1)} %copy-done, bf16[2048,128]{1,0:T(8,128)(2,1)S(1)} %collective-permute-done.4.visiting, ...), custom_call_target="tpu_custom_call" | custom-call | flops 6442450944 | bytes 4194304 | tf_op jit(solution)/shard_map/pallas_call | solution.py:213
  84.4 0.1 collective-permute-start.6
  84.5 0.0 collective-permute-done.8
  84.5 0.1 add.22
  84.6 1.2 %collective-permute-start.9 = (f32[1024,128]{1,0:T(8,128)S(1)}, f32[1024,128]{1,0:T(8,128)S(1)}, u32[]{:S(2)}, u32[]{:S(2)}) collective-permute-start(f32[1024,128]{1,0:T(8,128)S(1)} %slice_bitcast_fusion), channel_id=1, source_target_pairs={{0,2},{1,3},{2,0},{3,1},{4,6},{5,7},{6,4},{7,5},{8,10},{9,11},{10,... | collective-permute-start | bytes 1572872 | tf_op jit(solution)/shard_map/ppermute | solution.py:27
  85.9 1.2 %collective-permute-done.6 = f32[2,1024,128]{2,1,0:T(8,128)S(1)} collective-permute-done((f32[2,1024,128]{2,1,0:T(8,128)S(1)}, f32[2,1024,128]{2,1,0:T(8,128)S(1)}, u32[]{:S(2)}, u32[]{:S(2)}) %collective-permute-start.6) | collective-permute-done | bytes 1048608 | tf_op jit(solution)/shard_map/ppermute | solution.py:27
  87.1 0.1 add.20
  87.3 1.2 %collective-permute-start.7 = (f32[1024,128]{1,0:T(8,128)S(1)}, f32[1024,128]{1,0:T(8,128)S(1)}, u32[]{:S(2)}, u32[]{:S(2)}) collective-permute-start(f32[1024,128]{1,0:T(8,128)S(1)} %slice_bitcast_fusion.2), channel_id=1, source_target_pairs={{0,2},{1,3},{2,0},{3,1},{4,6},{5,7},{6,4},{7,5},{8,10},{9,11},{10,... | collective-permute-start | bytes 1572872 | tf_op jit(solution)/shard_map/ppermute | solution.py:27
  88.5 9.2 %collective-permute-done.9 = f32[1024,128]{1,0:T(8,128)S(1)} collective-permute-done((f32[1024,128]{1,0:T(8,128)S(1)}, f32[1024,128]{1,0:T(8,128)S(1)}, u32[]{:S(2)}, u32[]{:S(2)}) %collective-permute-start.9) | collective-permute-done | bytes 524320 | tf_op jit(solution)/shard_map/ppermute | solution.py:27
  97.7 0.8 fusion
  98.6 10.4 %collective-permute-done.7 = f32[1024,128]{1,0:T(8,128)S(1)} collective-permute-done((f32[1024,128]{1,0:T(8,128)S(1)}, f32[1024,128]{1,0:T(8,128)S(1)}, u32[]{:S(2)}, u32[]{:S(2)}) %collective-permute-start.7) | collective-permute-done | bytes 524320 | tf_op jit(solution)/shard_map/ppermute | solution.py:27
  109.0 0.8 fusion.1
  (2 shorter events, 0.1 us)
Async XLA Ops:
  0.6 13.3 %copy-start.1 = (s32[2048]{0:T(1024)S(1)}, s32[2048]{0:T(1024)}, u32[]{:S(2)}) copy-start(s32[2048]{0:T(1024)} %param.13) | copy-start | bytes 24580
  0.6 13.3 %copy-start = (bf16[2048,128]{1,0:T(8,128)(2,1)S(1)}, bf16[2048,128]{1,0:T(8,128)(2,1)}, u32[]{:S(2)}) copy-start(bf16[2048,128]{1,0:T(8,128)(2,1)} %acc.7) | copy-start | bytes 1572868
  0.7 10.6 %copy-start.2 = (bf16[2048,128]{1,0:T(8,128)(2,1)S(1)}, bf16[2048,128]{1,0:T(8,128)(2,1)}, u32[]{:S(2)}) copy-start(bf16[2048,128]{1,0:T(8,128)(2,1)} %merch.7) | copy-start | bytes 1572868
  3.3 34.7 %collective-permute-start.3 = (bf16[2080,128]{1,0:T(8,128)(2,1)}, bf16[2080,128]{1,0:T(8,128)(2,1)S(1)}, u32[]{:S(2)}, u32[]{:S(2)}) collective-permute-start(bf16[2080,128]{1,0:T(8,128)(2,1)} %pad_maximum_fusion), channel_id=1, source_target_pairs={{8,0},{12,4},{16,8},{20,12},{24,16},{28,20},{32,24},{36,28},{40,32... | collective-permute-start | bytes 1597448 | tf_op jit(solution)/shard_map/ppermute | solution.py:23
  9.5 39.0 %collective-permute-start.1 = (bf16[2080,128]{1,0:T(8,128)(2,1)}, bf16[2080,128]{1,0:T(8,128)(2,1)S(1)}, u32[]{:S(2)}, u32[]{:S(2)}) collective-permute-start(bf16[2080,128]{1,0:T(8,128)(2,1)} %pad_maximum_fusion), channel_id=1, source_target_pairs={{4,0},{8,4},{12,8},{16,12},{20,16},{24,20},{28,24},{32,28},{36,32}... | collective-permute-start | bytes 1597448 | tf_op jit(solution)/shard_map/ppermute | solution.py:23
  11.2 26.8 %collective-permute-start.2 = (bf16[2048,128]{1,0:T(8,128)(2,1)S(1)}, bf16[2048,128]{1,0:T(8,128)(2,1)S(1)}, u32[]{:S(2)}, u32[]{:S(2)}) collective-permute-start(bf16[2048,128]{1,0:T(8,128)(2,1)S(1)} %copy-done.2), channel_id=1, source_target_pairs={{120,0},{124,4},{0,8},{4,12},{8,16},{12,20},{16,24},{20,28},{24,32... | collective-permute-start | bytes 1572872 | tf_op jit(solution)/shard_map/ppermute | solution.py:23
  12.6 35.9 %collective-permute-start = (bf16[2048,128]{1,0:T(8,128)(2,1)S(1)}, bf16[2048,128]{1,0:T(8,128)(2,1)S(1)}, u32[]{:S(2)}, u32[]{:S(2)}) collective-permute-start(bf16[2048,128]{1,0:T(8,128)(2,1)S(1)} %copy-done.2), channel_id=1, source_target_pairs={{124,0},{0,4},{4,8},{8,12},{12,16},{16,20},{20,24},{24,28},{28,32}... | collective-permute-start | bytes 1572872 | tf_op jit(solution)/shard_map/ppermute | solution.py:23
  48.5 15.1 %copy-start.3 = (s32[2048]{0:T(1024)S(1)}, s32[2048]{0:T(1024)}, u32[]{:S(2)}) copy-start(s32[2048]{0:T(1024)} %param.15) | copy-start | bytes 24580
  48.5 15.1 %copy-start.5 = (s32[16,1]{0,1:T(1,128)S(1)}, s32[16,1]{0,1:T(1,128)}, u32[]{:S(2)}) copy-start(s32[16,1]{0,1:T(1,128)} %param.17) | copy-start | bytes 196
  48.5 15.0 %collective-permute-start.5 = (bf16[2080,128]{1,0:T(8,128)(2,1)S(1)}, bf16[2080,128]{1,0:T(8,128)(2,1)S(1)}, u32[]{:S(2)}, u32[]{:S(2)}) collective-permute-start(bf16[2080,128]{1,0:T(8,128)(2,1)S(1)} %collective-permute-done.1.guest), channel_id=1, source_target_pairs={{8,0},{12,4},{16,8},{20,12},{24,16},{28,20},{32,24},{36,28},{40,32... | collective-permute-start | bytes 1597448 | tf_op jit(solution)/shard_map/ppermute | solution.py:23
  48.6 15.0 %collective-permute-start.4 = (bf16[2048,128]{1,0:T(8,128)(2,1)S(1)}, bf16[2048,128]{1,0:T(8,128)(2,1)S(1)}, u32[]{:S(2)}, u32[]{:S(2)}) collective-permute-start(bf16[2048,128]{1,0:T(8,128)(2,1)S(1)} %collective-permute-done.visiting), channel_id=1, source_target_pairs={{120,0},{124,4},{0,8},{4,12},{8,16},{12,20},{16,24},{20,28},{24,32... | collective-permute-start | bytes 1572872 | tf_op jit(solution)/shard_map/ppermute | solution.py:23
  63.6 12.0 %copy-start.4 = (s32[2048]{0:T(1024)S(1)}, s32[2048]{0:T(1024)}, u32[]{:S(2)}) copy-start(s32[2048]{0:T(1024)} %param.14) | copy-start | bytes 24580
  63.6 12.0 %copy-start.6 = (s32[16,1]{0,1:T(1,128)S(1)}, s32[16,1]{0,1:T(1,128)}, u32[]{:S(2)}) copy-start(s32[16,1]{0,1:T(1,128)} %param.16) | copy-start | bytes 196
  72.3 12.2 %collective-permute-start.8 = (f32[2,1024,128]{2,1,0:T(8,128)S(1)}, f32[2,1024,128]{2,1,0:T(8,128)S(1)}, u32[]{:S(2)}, u32[]{:S(2)}) collective-permute-start(f32[2,1024,128]{2,1,0:T(8,128)S(1)} %get-tuple-element.25), channel_id=1, source_target_pairs={{0,1},{1,0},{2,3},{3,2},{4,5},{5,4},{6,7},{7,6},{8,9},{9,8},{10,11... | collective-permute-start | bytes 3145736 | tf_op jit(solution)/shard_map/ppermute | solution.py:27
  84.4 2.7 %collective-permute-start.6 = (f32[2,1024,128]{2,1,0:T(8,128)S(1)}, f32[2,1024,128]{2,1,0:T(8,128)S(1)}, u32[]{:S(2)}, u32[]{:S(2)}) collective-permute-start(f32[2,1024,128]{2,1,0:T(8,128)S(1)} %get-tuple-element.22), channel_id=1, source_target_pairs={{0,1},{1,0},{2,3},{3,2},{4,5},{5,4},{6,7},{7,6},{8,9},{9,8},{10,11... | collective-permute-start | bytes 3145736 | tf_op jit(solution)/shard_map/ppermute | solution.py:27
  84.6 13.1 %collective-permute-start.9 = (f32[1024,128]{1,0:T(8,128)S(1)}, f32[1024,128]{1,0:T(8,128)S(1)}, u32[]{:S(2)}, u32[]{:S(2)}) collective-permute-start(f32[1024,128]{1,0:T(8,128)S(1)} %slice_bitcast_fusion), channel_id=1, source_target_pairs={{0,2},{1,3},{2,0},{3,1},{4,6},{5,7},{6,4},{7,5},{8,10},{9,11},{10,... | collective-permute-start | bytes 1572872 | tf_op jit(solution)/shard_map/ppermute | solution.py:27
  87.3 21.7 %collective-permute-start.7 = (f32[1024,128]{1,0:T(8,128)S(1)}, f32[1024,128]{1,0:T(8,128)S(1)}, u32[]{:S(2)}, u32[]{:S(2)}) collective-permute-start(f32[1024,128]{1,0:T(8,128)S(1)} %slice_bitcast_fusion.2), channel_id=1, source_target_pairs={{0,2},{1,3},{2,0},{3,1},{4,6},{5,7},{6,4},{7,5},{8,10},{9,11},{10,... | collective-permute-start | bytes 1572872 | tf_op jit(solution)/shard_map/ppermute | solution.py:27
